TPU v7x, 32 devices: a whole 2x2x4 slice. The times are simulated.
32 devices in a mesh: groups: 2 (over x), seq: 16 (over z, y, core).
Axes of the slice: x: 2, y: 2, z: 4, core: 2. Of those that a mesh axis runs over, the one named last changes fastest.
Arguments:
- lengths: int32 [24], P('groups'), parts along dimension 0, may hold values from 1 to 4, as said below
- query: bfloat16 [4096, 4096], P(('groups', 'seq')), parts along dimension 0
- keys: bfloat16 [4096, 1024], P(('groups', 'seq')), parts along dimension 0
- values: bfloat16 [4096, 1024], P(('groups', 'seq')), parts along dimension 0, may hold values from -6 to 6
- new_query: bfloat16 [24, 4096], P('groups'), parts along dimension 0
- new_key: bfloat16 [24, 1024], P('groups'), parts along dimension 0
- new_value: bfloat16 [24, 1024], P('groups'), parts along dimension 0, may hold values from -6 to 6
Outputs:
- prefill: bfloat16 [4096, 4096], P(('groups', 'seq')), parts along dimension 0
- decoded: bfloat16 [24, 4096], P('groups'), parts along dimension 0
There are 2 independent parts, one for each index of `groups`. A program takes and returns all parts, laid end to end along the dimension named above; each array names one. Nothing has to cross between parts.
Inputs may be any that keep to these rules, and one draw needn't show every extreme that they name: Each prompt covers 1 to 4 whole devices, the lengths sum to 16, and one prompt covers exactly 4.
All inputs are finite; a program needn't handle non-finite values.
Results may differ from a plain program's by a relative error of at most 0.0075.
Values may be sent and summed in bfloat16 or wider, within the bound.
A program may use at most 128 MiB of HBM per device.

v0:
```python
import functools
import math

import jax
import jax.numpy as jnp
from jax import lax
from jax.experimental import pallas as pl
from jax.experimental.pallas import tpu as pltpu
from jax.sharding import PartitionSpec as P

HEAD_DIM = 128
LOW = -1e30
HIGH = 3e38
AHEAD = 3


def body(lengths, query, keys, values, new_query, new_key, new_value):
    n_seq = lax.axis_size("seq")
    reach = n_seq // 4
    half = reach // 2
    tok = query.shape[0]
    hd = HEAD_DIM
    heads = query.shape[1] // hd
    kvh = keys.shape[1] // hd
    group = heads // kvh
    prompts = new_query.shape[0]
    span = reach * tok
    coef = math.log2(math.e) / math.sqrt(hd)
    quads = n_seq // 4
    f32, bf16 = jnp.float32, jnp.bfloat16

    def kernel(len_ref, q_hbm, k_hbm, v_hbm, nq_ref, nk_ref, nv_ref, out_hbm, dec_ref,
               qbuf, kvb, obuf, dbuf, qd, nk32, nv32, oall, tri,
               load_sem, q_sem, out_sem, send_sem, fwd_sem, recv_sem, d_send, d_recv):
        me = lax.axis_index("seq")
        core = lax.rem(me, 2)
        sibling = me + 1 - 2 * core

        def load_copies(h):
            return [
                pltpu.make_async_copy(
                    src.at[:, pl.ds(h * hd, hd)],
                    kvb.at[h, part, pl.ds((reach - 1) * tok, tok), :],
                    load_sem.at[h, part],
                )
                for part, src in enumerate((k_hbm, v_hbm))
            ]

        for h in range(kvh):
            for copy in load_copies(h):
                copy.start()
        q_copy = pltpu.make_async_copy(q_hbm, qbuf, q_sem)
        q_copy.start()

        barrier = pltpu.get_barrier_semaphore()
        for k in range(1, n_seq):
            pl.semaphore_signal(barrier, inc=1, device_id={"seq": lax.rem(me + k, n_seq)},
                                device_id_type=pl.DeviceIdType.MESH)

        run = jnp.int32(0)
        first_dev, pid, is_last = jnp.int32(0), jnp.int32(0), jnp.int32(0)
        starts, sizes = [], []
        for p in range(prompts):
            size = len_ref[p]
            starts.append(run)
            sizes.append(size)
            inside = (run <= me) & (me < run + size)
            first_dev = jnp.where(inside, run, first_dev)
            pid = jnp.where(inside, p, pid)
            is_last = jnp.where(inside & (me == run + size - 1), 1, is_last)
            run = run + size

        rows = lax.broadcasted_iota(jnp.int32, (tok, tok), 0)
        cols = lax.broadcasted_iota(jnp.int32, (tok, tok), 1)
        tri[...] = jnp.where(cols <= rows, HIGH, LOW)

        def slot(d):
            return pl.ds((reach - 1 - d) * tok, tok)

        for d in range(1, reach):
            @pl.when(me < d)
            def _(d=d):
                kvb[:, :, slot(d), :] = jnp.zeros((kvh, 2, tok, hd), bf16)

        for h in range(kvh):
            for copy in load_copies(h):
                copy.wait()
        pl.semaphore_wait(barrier, n_seq - 1)

        def remote(h, held, put, sem, target):
            return pltpu.make_async_remote_copy(
                src_ref=kvb.at[h, :, pl.ds(held * tok, tok), :],
                dst_ref=kvb.at[h, :, pl.ds(put * tok, tok), :],
                send_sem=sem,
                recv_sem=recv_sem.at[h, put],
                device_id={"seq": target},
                device_id_type=pl.DeviceIdType.MESH,
            )

        own = reach - 1

        def each_send(h, act):
            @pl.when(core == 0)
            def _():
                act(remote(h, own, reach - 2, send_sem.at[h, half - 1], me + 1))
            for j in range(1, half):
                @pl.when(me + 2 * j < n_seq)
                def _(j=j):
                    act(remote(h, own, own - 2 * j, send_sem.at[h, j - 1], me + 2 * j))
            @pl.when((core == 1) & (me + reach - 1 < n_seq))
            def _():
                act(remote(h, own, 0, send_sem.at[h, half - 1], me + reach - 1))

        def each_forward(h, act, arrive):
            for j in range(1, half):
                @pl.when(me >= 2 * j)
                def _(j=j):
                    put = own - 2 * j - 1 + 2 * core
                    copy = remote(h, own - 2 * j, put, fwd_sem.at[h, j - 1], sibling)
                    if arrive:
                        remote(h, own, own - 2 * j, fwd_sem.at[h, j - 1], sibling).wait_recv()
                    act(copy)

        def wait_rest(h):
            for j in range(half):
                @pl.when(me >= 2 * j + 1)
                def _(j=j):
                    remote(h, own, own - 2 * j - 1, fwd_sem.at[h, 0], sibling).wait_recv()

        start = lambda c: c.start()
        wait_send = lambda c: c.wait_send()
        for h in range(min(AHEAD, kvh)):
            each_send(h, start)

        picked = lax.broadcasted_iota(jnp.int32, (prompts, hd), 0) == pid

        def pick(ref, h):
            block = ref[:, h * hd:(h + 1) * hd].astype(f32)
            return jnp.sum(jnp.where(picked, block, 0.0), axis=0, keepdims=True)

        for h in range(heads):
            qd[h:h + 1, :] = pick(nq_ref, h)
        for h in range(kvh):
            nk32[h * group:(h + 1) * group, :] = jnp.broadcast_to(pick(nk_ref, h), (group, hd))
            nv32[h * group:(h + 1) * group, :] = jnp.broadcast_to(pick(nv_ref, h), (group, hd))
        q32 = qd[...]
        q32b = q32.astype(bf16)
        row_head = lax.broadcasted_iota(jnp.int32, (heads, tok), 0) // group
        own_rows = pl.ds((reach - 1) * tok, tok)
        contract_last = (((1,), (1,)), ((), ()))
        scores = jnp.zeros((heads, tok), f32)
        for h in range(kvh):
            part = lax.dot_general(q32b, kvb[h, 0, own_rows, :], contract_last,
                                   preferred_element_type=f32)
            scores = jnp.where(row_head == h, part, scores)
        own_score = jnp.sum(q32 * nk32[...], axis=1, keepdims=True)
        own_score = jnp.where(is_last == 1, own_score, LOW)
        peak = jnp.maximum(jnp.max(scores, axis=1, keepdims=True), own_score)
        weights = jnp.exp2((scores - peak) * coef)
        own_weight = jnp.exp2((own_score - peak) * coef)
        total = jnp.sum(weights, axis=1, keepdims=True) + own_weight
        accum = own_weight.astype(bf16).astype(f32) * nv32[...]
        for h in range(kvh):
            masked = jnp.where(row_head == h, weights, 0.0).astype(bf16)
            accum += jnp.dot(masked, kvb[h, 1, own_rows, :], preferred_element_type=f32)

        quad = me // 4
        side = lax.rem(me // 2, 2)
        dbuf[quad, core, side, 0:heads, :] = accum / total
        dbuf[quad, core, side, heads:, :] = jnp.broadcast_to(
            peak * coef + jnp.log2(total), (heads, hd))

        def d_copy(ref, send, recv, target):
            return pltpu.make_async_remote_copy(
                src_ref=ref, dst_ref=ref, send_sem=d_send.at[send], recv_sem=d_recv.at[recv],
                device_id={"seq": target}, device_id_type=pl.DeviceIdType.MESH)

        across = me + 2 - 4 * side
        d_first = d_copy(dbuf.at[quad, core, side], 0, 0, across)
        d_first_in = d_copy(dbuf.at[quad, core, 1 - side], 0, 0, across)
        d_far = [d_copy(dbuf.at[quad, core], k, k, lax.rem(me + 4 * k, n_seq))
                 for k in range(1, quads)]
        d_far_in = [d_copy(dbuf.at[lax.rem(quad + quads - k, quads), core], k, k, sibling)
                    for k in range(1, quads)]
        d_last = d_copy(dbuf.at[:, core], quads, quads, sibling)
        d_last_in = d_copy(dbuf.at[:, 1 - core], quads, quads, sibling)

        d_first.start()
        q_copy.wait()

        block_of = lax.broadcasted_iota(jnp.int32, (1, span - tok), 1) // tok
        cap = jnp.where(me - (reach - 1) + block_of >= first_dev, HIGH, LOW)

        def out_copy(h):
            at = pl.ds(pl.multiple_of(h * group * hd, hd), group * hd)
            return pltpu.make_async_copy(obuf.at[:, at], out_hbm.at[:, at], out_sem.at[h])

        def attend(h):
            k_all = kvb[h, 0]
            v_all = kvb[h, 1]
            for g in range(group):
                at = pl.ds(pl.multiple_of((h * group + g) * hd, hd), hd)
                s = lax.dot_general(qbuf[:, at], k_all, contract_last,
                                    preferred_element_type=f32)
                far = jnp.minimum(s[:, :span - tok], cap)
                near = jnp.minimum(s[:, span - tok:], tri[...])
                top = jnp.maximum(jnp.max(far, axis=1, keepdims=True),
                                  jnp.max(near, axis=1, keepdims=True))
                w = jnp.exp2((jnp.concatenate([far, near], axis=1) - top) * coef)
                tot = jnp.sum(w, axis=1, keepdims=True)
                o = jnp.dot(w.astype(bf16), v_all, preferred_element_type=f32)
                obuf[:, at] = (o * (1.0 / tot)).astype(bf16)
            out_copy(h).start()

        def combine():
            d_last_in.wait_recv()
            for p in range(prompts):
                parts = []
                for k in range(reach):
                    d = jnp.minimum(starts[p] + k, n_seq - 1)
                    a, b, c = d // 4, lax.rem(d, 2), lax.rem(d // 2, 2)
                    lse = jnp.where(k < sizes[p], dbuf[a, b, c, heads:, :], LOW)
                    parts.append((lse, a, b, c))
                m = functools.reduce(jnp.maximum, [x[0] for x in parts])
                num = jnp.zeros((heads, hd), f32)
                den = jnp.zeros((heads, hd), f32)
                for lse, a, b, c in parts:
                    w = jnp.exp2(lse - m)
                    den += w
                    num += w * dbuf[a, b, c, 0:heads, :]
                oall[p * heads:(p + 1) * heads, :] = num / den
            for h in range(heads):
                dec_ref[:, h * hd:(h + 1) * hd] = oall[
                    pl.ds(h, prompts, stride=heads), :].astype(bf16)

        far_at = min(2, kvh - 1)
        last_at = min(5, kvh - 1)

        def step(h, carry):
            @pl.when(h + AHEAD < kvh)
            def _():
                each_send(h + AHEAD, start)

            @pl.when(h == far_at)
            def _():
                d_first_in.wait_recv()
                for c in d_far:
                    c.start()

            @pl.when(h == last_at)
            def _():
                for c in d_far_in:
                    c.wait_recv()
                d_last.start()

            @pl.when(h == kvh - 1)
            def _():
                combine()

            each_forward(h, start, True)

            @pl.when(h >= 1)
            def _():
                wait_rest(h - 1)
                attend(h - 1)
            return carry

        lax.fori_loop(0, kvh, step, 0)
        wait_rest(kvh - 1)
        attend(kvh - 1)

        d_first.wait_send()
        for c in d_far:
            c.wait_send()
        d_last.wait_send()

        def drain(h, carry):
            each_send(h, wait_send)
            each_forward(h, wait_send, False)
            out_copy(h).wait()
            return carry

        lax.fori_loop(0, kvh, drain, 0)

    any_spec = pl.BlockSpec(memory_space=pl.ANY)
    vmem = pl.BlockSpec(memory_space=pltpu.VMEM)
    return pl.pallas_call(
        kernel,
        out_shape=(
            jax.ShapeDtypeStruct((tok, heads * hd), bf16),
            jax.ShapeDtypeStruct((prompts, heads * hd), bf16),
        ),
        in_specs=[pl.BlockSpec(memory_space=pltpu.SMEM)] + [any_spec] * 3 + [vmem] * 3,
        out_specs=(any_spec, vmem),
        scratch_shapes=[
            pltpu.VMEM((tok, heads * hd), bf16),
            pltpu.VMEM((kvh, 2, span, hd), bf16),
            pltpu.VMEM((tok, heads * hd), bf16),
            pltpu.VMEM((quads, 2, 2, 2 * heads, hd), f32),
            pltpu.VMEM((heads, hd), f32),
            pltpu.VMEM((heads, hd), f32),
            pltpu.VMEM((heads, hd), f32),
            pltpu.VMEM((prompts * heads, hd), f32),
            pltpu.VMEM((tok, tok), f32),
            pltpu.SemaphoreType.DMA((kvh, 2)),
            pltpu.SemaphoreType.DMA,
            pltpu.SemaphoreType.DMA((kvh,)),
            pltpu.SemaphoreType.DMA((kvh, half)),
            pltpu.SemaphoreType.DMA((kvh, half)),
            pltpu.SemaphoreType.DMA((kvh, reach)),
            pltpu.SemaphoreType.DMA((quads + 1,)),
            pltpu.SemaphoreType.DMA((quads + 1,)),
        ],
        compiler_params=pltpu.CompilerParams(
            collective_id=0, has_side_effects=True, vmem_limit_bytes=56 * 1024 * 1024
        ),
    )(lengths, query, keys, values, new_query, new_key, new_value)


def solution(mesh):
    in_specs = (
        P("groups"),
        P(("groups", "seq"), None),
        P(("groups", "seq"), None),
        P(("groups", "seq"), None),
        P("groups", None),
        P("groups", None),
        P("groups", None),
    )
    out_specs = (P(("groups", "seq"), None), P("groups", None))
    return jax.shard_map(body, mesh=mesh, in_specs=in_specs, out_specs=out_specs, check_vma=False)
```

profile of v0, /device:TPU:17, one launch (start us, length us, event | category | flops | bytes accessed | tf_op | source)
XLA Modules:
  0.0 36.6 jit_solution(230607641353481492)
XLA Ops:
  0.6 33.0 %shard_map.86 = (bf16[128,4096]{1,0:T(8,128)(2,1)}, bf16[12,4096]{1,0:T(8,128)(2,1)}) custom-call(s32[12]{0:T(128)} %len_ref.1, bf16[128,4096]{1,0:T(8,128)(2,1)} %q_hbm.1, bf16[128,1024]{1,0:T(8,128)(2,1)} %k_hbm.1, bf16[128,1024]{1,0:T(8,128)(2,1)} %v_hbm.1, bf16[12,4096]{1,0:T(8,128)(2,1)} %nq_ref.1, bf16[12,1024]{1,0:T(8,128)(2,1)} %nk_ref.1, ...), custom_call_target="tpu_custom_call" | custom-call | tf_op jit(solution)/shard_map/pallas_call | solution.py:287
  33.6 0.0 copy-start
  33.6 2.3 %copy.11 = bf16[128,4096]{1,0:T(8,128)(2,1)} copy(bf16[128,4096]{1,0:T(8,128)(2,1)} %get-tuple-element.4) | data formatting | bytes 2097152
  35.9 0.0 copy-done
  35.9 0.7 %copy.12 = bf16[12,4096]{1,0:T(8,128)(2,1)} copy(bf16[12,4096]{1,0:T(8,128)(2,1)S(1)} %copy-done) | data formatting | bytes 196608
Async XLA Ops:
  33.6 2.3 %copy-start = (bf16[12,4096]{1,0:T(8,128)(2,1)S(1)}, bf16[12,4096]{1,0:T(8,128)(2,1)}, u32[]{:S(2)}) copy-start(bf16[12,4096]{1,0:T(8,128)(2,1)} %get-tuple-element.5) | copy-start | bytes 294916
where the time goes:
time: 36.8 us; the launch traced here: 36.6 us
  Pallas kernels  33 us (90%)
  local copies, waits for them, and re-layouts  2.98 us (8%)
  between operations  0.65 us (2%)
    pallas_call x1, Pallas kernels, body(): pl.pallas_call(kernel, out_shape=(jax.ShapeDtypeStruct((tok, heads * hd),...  33 us
    unnamed x4, local copies, waits for them, and re-layouts  2.98 us

commit v1 on v0

--- a/solution.py
+++ b/solution.py
@@ -12,6 +12,7 @@
 LOW = -1e30
 HIGH = 3e38
 AHEAD = 3
+LEAD = 2
 
 
 def body(lengths, query, keys, values, new_query, new_key, new_value):
@@ -29,9 +30,9 @@
     quads = n_seq // 4
     f32, bf16 = jnp.float32, jnp.bfloat16
 
-    def kernel(len_ref, q_hbm, k_hbm, v_hbm, nq_ref, nk_ref, nv_ref, out_hbm, dec_ref,
-               qbuf, kvb, obuf, dbuf, qd, nk32, nv32, oall, tri,
-               load_sem, q_sem, out_sem, send_sem, fwd_sem, recv_sem, d_send, d_recv):
+    def kernel(len_ref, q_hbm, k_hbm, v_hbm, nq_ref, nk_ref, nv_ref, out_ref, dec_ref,
+               qbuf, kvb, dbuf, qd, nk32, nv32, oall, lall, tri,
+               load_sem, q_sem, send_sem, fwd_sem, relay_sem, recv_sem, d_send, d_recv):
         me = lax.axis_index("seq")
         core = lax.rem(me, 2)
         sibling = me + 1 - 2 * core
@@ -99,17 +100,31 @@
 
         own = reach - 1
 
+        odd = lax.rem(me // 2, 2)
+        relayed = (core == 1) & (odd == 1) if half == 2 else (core == 2)
+        relays = (core == 0) & (odd == 1) & (me >= reach - 1) if half == 2 else (core == 2)
+
+        def each_near(h, act):
+            @pl.when(core == 0)
+            def _():
+                act(remote(h, own, reach - 2, send_sem.at[h, half - 1], me + 1))
+            @pl.when((core == 1) & (me + reach - 1 < n_seq))
+            def _():
+                act(remote(h, own, 0, send_sem.at[h, half - 1], me + reach - 1))
+
         def each_send(h, act):
-            @pl.when(core == 0)
-            def _():
-                act(remote(h, own, reach - 2, send_sem.at[h, half - 1], me + 1))
             for j in range(1, half):
-                @pl.when(me + 2 * j < n_seq)
+                @pl.when((me + 2 * j < n_seq) & jnp.logical_not(relayed))
                 def _(j=j):
                     act(remote(h, own, own - 2 * j, send_sem.at[h, j - 1], me + 2 * j))
-            @pl.when((core == 1) & (me + reach - 1 < n_seq))
-            def _():
-                act(remote(h, own, 0, send_sem.at[h, half - 1], me + reach - 1))
+
+        def each_relay(h, act, arrive):
+            if half == 2:
+                @pl.when(relays)
+                def _():
+                    if arrive:
+                        remote(h, own, 0, relay_sem.at[h], sibling).wait_recv()
+                    act(remote(h, 0, own - 2, relay_sem.at[h], me - 1))
 
         def each_forward(h, act, arrive):
             for j in range(1, half):
@@ -123,14 +138,19 @@
 
         def wait_rest(h):
             for j in range(half):
-                @pl.when(me >= 2 * j + 1)
+                here = me >= 2 * j + 1
+                if j == half - 1:
+                    here = here & jnp.logical_not(relays)
+                @pl.when(here)
                 def _(j=j):
                     remote(h, own, own - 2 * j - 1, fwd_sem.at[h, 0], sibling).wait_recv()
 
         start = lambda c: c.start()
         wait_send = lambda c: c.wait_send()
-        for h in range(min(AHEAD, kvh)):
-            each_send(h, start)
+        for h in range(kvh):
+            each_near(h, start)
+            if h < AHEAD:
+                each_send(h, start)
 
         picked = lax.broadcasted_iota(jnp.int32, (prompts, hd), 0) == pid
 
@@ -167,8 +187,11 @@
         quad = me // 4
         side = lax.rem(me // 2, 2)
         dbuf[quad, core, side, 0:heads, :] = accum / total
+        diag = (lax.broadcasted_iota(jnp.int32, (heads, hd), 0)
+                == lax.broadcasted_iota(jnp.int32, (heads, hd), 1))
+        level = jnp.where(diag, peak * coef + jnp.log2(total), 0.0)
         dbuf[quad, core, side, heads:, :] = jnp.broadcast_to(
-            peak * coef + jnp.log2(total), (heads, hd))
+            jnp.sum(level, axis=0, keepdims=True), (8, hd))
 
         def d_copy(ref, send, recv, target):
             return pltpu.make_async_remote_copy(
@@ -190,10 +213,6 @@
 
         block_of = lax.broadcasted_iota(jnp.int32, (1, span - tok), 1) // tok
         cap = jnp.where(me - (reach - 1) + block_of >= first_dev, HIGH, LOW)
-
-        def out_copy(h):
-            at = pl.ds(pl.multiple_of(h * group * hd, hd), group * hd)
-            return pltpu.make_async_copy(obuf.at[:, at], out_hbm.at[:, at], out_sem.at[h])
 
         def attend(h):
             k_all = kvb[h, 0]
@@ -209,17 +228,19 @@
                 w = jnp.exp2((jnp.concatenate([far, near], axis=1) - top) * coef)
                 tot = jnp.sum(w, axis=1, keepdims=True)
                 o = jnp.dot(w.astype(bf16), v_all, preferred_element_type=f32)
-                obuf[:, at] = (o * (1.0 / tot)).astype(bf16)
-            out_copy(h).start()
+                out_ref[:, at] = (o * (1.0 / tot)).astype(bf16)
 
         def combine():
             d_last_in.wait_recv()
+            for d in range(n_seq):
+                level = jnp.where(diag, dbuf[d // 4, d % 2, d // 2 % 2, heads:heads + 1, :], 0.0)
+                lall[d] = jnp.broadcast_to(jnp.sum(level, axis=1, keepdims=True), (heads, hd))
             for p in range(prompts):
                 parts = []
                 for k in range(reach):
                     d = jnp.minimum(starts[p] + k, n_seq - 1)
                     a, b, c = d // 4, lax.rem(d, 2), lax.rem(d // 2, 2)
-                    lse = jnp.where(k < sizes[p], dbuf[a, b, c, heads:, :], LOW)
+                    lse = jnp.where(k < sizes[p], lall[d], LOW)
                     parts.append((lse, a, b, c))
                 m = functools.reduce(jnp.maximum, [x[0] for x in parts])
                 num = jnp.zeros((heads, hd), f32)
@@ -257,6 +278,10 @@
             def _():
                 combine()
 
+            @pl.when(h + LEAD < kvh)
+            def _():
+                each_relay(h + LEAD, start, True)
+
             each_forward(h, start, True)
 
             @pl.when(h >= 1)
@@ -265,6 +290,8 @@
                 attend(h - 1)
             return carry
 
+        for h in range(min(LEAD, kvh)):
+            each_relay(h, start, True)
         lax.fori_loop(0, kvh, step, 0)
         wait_rest(kvh - 1)
         attend(kvh - 1)
@@ -276,8 +303,9 @@
 
         def drain(h, carry):
             each_send(h, wait_send)
+            each_near(h, wait_send)
             each_forward(h, wait_send, False)
-            out_copy(h).wait()
+            each_relay(h, wait_send, False)
             return carry
 
         lax.fori_loop(0, kvh, drain, 0)
@@ -287,26 +315,26 @@
     return pl.pallas_call(
         kernel,
         out_shape=(
-            jax.ShapeDtypeStruct((tok, heads * hd), bf16),
-            jax.ShapeDtypeStruct((prompts, heads * hd), bf16),
+            pltpu.VMEM((tok, heads * hd), bf16),
+            pltpu.VMEM((prompts, heads * hd), bf16),
         ),
         in_specs=[pl.BlockSpec(memory_space=pltpu.SMEM)] + [any_spec] * 3 + [vmem] * 3,
-        out_specs=(any_spec, vmem),
+        out_specs=(vmem, vmem),
         scratch_shapes=[
             pltpu.VMEM((tok, heads * hd), bf16),
             pltpu.VMEM((kvh, 2, span, hd), bf16),
-            pltpu.VMEM((tok, heads * hd), bf16),
-            pltpu.VMEM((quads, 2, 2, 2 * heads, hd), f32),
+            pltpu.VMEM((quads, 2, 2, heads + 8, hd), f32),
             pltpu.VMEM((heads, hd), f32),
             pltpu.VMEM((heads, hd), f32),
             pltpu.VMEM((heads, hd), f32),
             pltpu.VMEM((prompts * heads, hd), f32),
+            pltpu.VMEM((n_seq, heads, hd), f32),
             pltpu.VMEM((tok, tok), f32),
             pltpu.SemaphoreType.DMA((kvh, 2)),
             pltpu.SemaphoreType.DMA,
-            pltpu.SemaphoreType.DMA((kvh,)),
             pltpu.SemaphoreType.DMA((kvh, half)),
             pltpu.SemaphoreType.DMA((kvh, half)),
+            pltpu.SemaphoreType.DMA((kvh,)),
             pltpu.SemaphoreType.DMA((kvh, reach)),
             pltpu.SemaphoreType.DMA((quads + 1,)),
             pltpu.SemaphoreType.DMA((quads + 1,)),

time: 36.8 us -> 29.6 us (0.80)
  the two profiles are of different devices: /device:TPU:17 before, /device:TPU:0 now
where the time goes in v1:
time: 29.6 us; the launch traced here: 29.5 us
  Pallas kernels  27.2 us (92%)
  local copies, waits for them, and re-layouts  1.63 us (6%)
  between operations  0.64 us (2%)
    pallas_call x1, Pallas kernels, body(): pl.pallas_call(kernel, out_shape=(pltpu.VMEM((tok, heads * hd), bf16), pl...  27.2 us
    unnamed x2, local copies, waits for them, and re-layouts  1.63 us

profile of v1, /device:TPU:0, one launch (start us, length us, event | category | flops | bytes accessed | tf_op | source)
XLA Modules:
  0.0 29.5 jit_solution(16752875350702913576)
XLA Ops:
  0.6 27.2 %shard_map.86 = (bf16[128,4096]{1,0:T(8,128)(2,1)S(1)}, bf16[12,4096]{1,0:T(8,128)(2,1)S(1)}) custom-call(s32[12]{0:T(128)} %len_ref.1, bf16[128,4096]{1,0:T(8,128)(2,1)} %q_hbm.1, bf16[128,1024]{1,0:T(8,128)(2,1)} %k_hbm.1, bf16[128,1024]{1,0:T(8,128)(2,1)} %v_hbm.1, bf16[12,4096]{1,0:T(8,128)(2,1)} %nq_ref.1, bf16[12,1024]{1,0:T(8,128)(2,1)} %nk_ref.1, ...), custom_call_target="tpu_custom_call" | custom-call | tf_op jit(solution)/shard_map/pallas_call | solution.py:315
  27.8 1.0 %copy.11 = bf16[128,4096]{1,0:T(8,128)(2,1)} copy(bf16[128,4096]{1,0:T(8,128)(2,1)S(1)} %get-tuple-element.2) | data formatting | bytes 2097152
  28.8 0.7 %copy.12 = bf16[12,4096]{1,0:T(8,128)(2,1)} copy(bf16[12,4096]{1,0:T(8,128)(2,1)S(1)} %get-tuple-element.3) | data formatting | bytes 196608

commit v2 on v1

--- a/solution.py
+++ b/solution.py
@@ -13,6 +13,7 @@
 HIGH = 3e38
 AHEAD = 3
 LEAD = 2
+PACK = 2
 
 
 def body(lengths, query, keys, values, new_query, new_key, new_value):
@@ -30,9 +31,9 @@
     quads = n_seq // 4
     f32, bf16 = jnp.float32, jnp.bfloat16
 
-    def kernel(len_ref, q_hbm, k_hbm, v_hbm, nq_ref, nk_ref, nv_ref, out_ref, dec_ref,
-               qbuf, kvb, dbuf, qd, nk32, nv32, oall, lall, tri,
-               load_sem, q_sem, send_sem, fwd_sem, relay_sem, recv_sem, d_send, d_recv):
+    def kernel(len_ref, q_hbm, k_hbm, v_hbm, nq_hbm, nk_hbm, nv_hbm, out_ref, dec_ref,
+               nq_ref, nk_ref, nv_ref, qbuf, kvb, dbuf, qd, nk32, nv32, oall, lall, tri,
+               load_sem, q_sem, n_sem, send_sem, fwd_sem, relay_sem, recv_sem, d_send, d_recv):
         me = lax.axis_index("seq")
         core = lax.rem(me, 2)
         sibling = me + 1 - 2 * core
@@ -51,6 +52,10 @@
             for copy in load_copies(h):
                 copy.start()
         q_copy = pltpu.make_async_copy(q_hbm, qbuf, q_sem)
+        n_copies = [pltpu.make_async_copy(src, dst, n_sem.at[n]) for n, (src, dst) in
+                    enumerate(((nq_hbm, nq_ref), (nk_hbm, nk_ref), (nv_hbm, nv_ref)))]
+        for copy in n_copies:
+            copy.start()
         q_copy.start()
 
         barrier = pltpu.get_barrier_semaphore()
@@ -71,21 +76,6 @@
             is_last = jnp.where(inside & (me == run + size - 1), 1, is_last)
             run = run + size
 
-        rows = lax.broadcasted_iota(jnp.int32, (tok, tok), 0)
-        cols = lax.broadcasted_iota(jnp.int32, (tok, tok), 1)
-        tri[...] = jnp.where(cols <= rows, HIGH, LOW)
-
-        def slot(d):
-            return pl.ds((reach - 1 - d) * tok, tok)
-
-        for d in range(1, reach):
-            @pl.when(me < d)
-            def _(d=d):
-                kvb[:, :, slot(d), :] = jnp.zeros((kvh, 2, tok, hd), bf16)
-
-        for h in range(kvh):
-            for copy in load_copies(h):
-                copy.wait()
         pl.semaphore_wait(barrier, n_seq - 1)
 
         def remote(h, held, put, sem, target):
@@ -148,10 +138,26 @@
         start = lambda c: c.start()
         wait_send = lambda c: c.wait_send()
         for h in range(kvh):
+            for copy in load_copies(h):
+                copy.wait()
             each_near(h, start)
             if h < AHEAD:
                 each_send(h, start)
 
+        rows = lax.broadcasted_iota(jnp.int32, (tok, tok), 0)
+        cols = lax.broadcasted_iota(jnp.int32, (tok, tok), 1)
+        tri[...] = jnp.where(cols <= rows, HIGH, LOW)
+
+        def slot(d):
+            return pl.ds((reach - 1 - d) * tok, tok)
+
+        for d in range(1, reach):
+            @pl.when(me < d)
+            def _(d=d):
+                kvb[:, :, slot(d), :] = jnp.zeros((kvh, 2, tok, hd), bf16)
+
+        for copy in n_copies:
+            copy.wait()
         picked = lax.broadcasted_iota(jnp.int32, (prompts, hd), 0) == pid
 
         def pick(ref, h):
@@ -217,18 +223,21 @@
         def attend(h):
             k_all = kvb[h, 0]
             v_all = kvb[h, 1]
-            for g in range(group):
-                at = pl.ds(pl.multiple_of((h * group + g) * hd, hd), hd)
-                s = lax.dot_general(qbuf[:, at], k_all, contract_last,
-                                    preferred_element_type=f32)
+            for g in range(0, group, PACK):
+                ats = [pl.ds(pl.multiple_of((h * group + g + n) * hd, hd), hd)
+                       for n in range(PACK)]
+                q = jnp.concatenate([qbuf[:, at] for at in ats], axis=0)
+                s = lax.dot_general(q, k_all, contract_last, preferred_element_type=f32)
                 far = jnp.minimum(s[:, :span - tok], cap)
-                near = jnp.minimum(s[:, span - tok:], tri[...])
-                top = jnp.maximum(jnp.max(far, axis=1, keepdims=True),
-                                  jnp.max(near, axis=1, keepdims=True))
-                w = jnp.exp2((jnp.concatenate([far, near], axis=1) - top) * coef)
+                near = jnp.minimum(s[:, span - tok:], jnp.concatenate([tri[...]] * PACK, axis=0))
+                s = jnp.concatenate([far, near], axis=1)
+                top = jnp.max(s, axis=1, keepdims=True)
+                w = jnp.exp2((s - top) * coef)
                 tot = jnp.sum(w, axis=1, keepdims=True)
                 o = jnp.dot(w.astype(bf16), v_all, preferred_element_type=f32)
-                out_ref[:, at] = (o * (1.0 / tot)).astype(bf16)
+                o = (o * (1.0 / tot)).astype(bf16)
+                for n, at in enumerate(ats):
+                    out_ref[:, at] = o[n * tok:(n + 1) * tok]
 
         def combine():
             d_last_in.wait_recv()
@@ -318,9 +327,12 @@
             pltpu.VMEM((tok, heads * hd), bf16),
             pltpu.VMEM((prompts, heads * hd), bf16),
         ),
-        in_specs=[pl.BlockSpec(memory_space=pltpu.SMEM)] + [any_spec] * 3 + [vmem] * 3,
+        in_specs=[pl.BlockSpec(memory_space=pltpu.SMEM)] + [any_spec] * 6,
         out_specs=(vmem, vmem),
         scratch_shapes=[
+            pltpu.VMEM(new_query.shape, bf16),
+            pltpu.VMEM(new_key.shape, bf16),
+            pltpu.VMEM(new_value.shape, bf16),
             pltpu.VMEM((tok, heads * hd), bf16),
             pltpu.VMEM((kvh, 2, span, hd), bf16),
             pltpu.VMEM((quads, 2, 2, heads + 8, hd), f32),
@@ -332,6 +344,7 @@
             pltpu.VMEM((tok, tok), f32),
             pltpu.SemaphoreType.DMA((kvh, 2)),
             pltpu.SemaphoreType.DMA,
+            pltpu.SemaphoreType.DMA((3,)),
             pltpu.SemaphoreType.DMA((kvh, half)),
             pltpu.SemaphoreType.DMA((kvh, half)),
             pltpu.SemaphoreType.DMA((kvh,)),

time: 29.6 us -> 27.2 us (0.919)
  Pallas kernels: 27.2 us -> 24.8 us
    pallas_call x1, Pallas kernels: 27.2 us -> 24.8 us  [body(): pl.pallas_call(kernel, out_shape=(pltpu.VMEM((tok, heads * hd), bf16), pl...]
where the time goes in v2:
time: 27.2 us; the launch traced here: 27 us
  Pallas kernels  24.8 us (91%)
  local copies, waits for them, and re-layouts  1.63 us (6%)
  between operations  0.64 us (2%)
    pallas_call x1, Pallas kernels, body(): pl.pallas_call(kernel, out_shape=(pltpu.VMEM((tok, heads * hd), bf16), pl...  24.8 us
    unnamed x2, local copies, waits for them, and re-layouts  1.63 us

profile of v2, /device:TPU:0, one launch (start us, length us, event | category | flops | bytes accessed | tf_op | source)
XLA Modules:
  0.0 27.0 jit_solution(3990970248271590778)
XLA Ops:
  0.6 24.8 %shard_map.86 = (bf16[128,4096]{1,0:T(8,128)(2,1)S(1)}, bf16[12,4096]{1,0:T(8,128)(2,1)S(1)}) custom-call(s32[12]{0:T(128)} %len_ref.1, bf16[128,4096]{1,0:T(8,128)(2,1)} %q_hbm.1, bf16[128,1024]{1,0:T(8,128)(2,1)} %k_hbm.1, bf16[128,1024]{1,0:T(8,128)(2,1)} %v_hbm.1, bf16[12,4096]{1,0:T(8,128)(2,1)} %nq_hbm.1, bf16[12,1024]{1,0:T(8,128)(2,1)} %nk_hbm.1, ...), custom_call_target="tpu_custom_call" | custom-call | tf_op jit(solution)/shard_map/pallas_call | solution.py:324
  25.4 1.0 %copy.11 = bf16[128,4096]{1,0:T(8,128)(2,1)} copy(bf16[128,4096]{1,0:T(8,128)(2,1)S(1)} %get-tuple-element.2) | data formatting | bytes 2097152
  26.4 0.7 %copy.12 = bf16[12,4096]{1,0:T(8,128)(2,1)} copy(bf16[12,4096]{1,0:T(8,128)(2,1)S(1)} %get-tuple-element.3) | data formatting | bytes 196608

commit v3 on v2

--- a/solution.py
+++ b/solution.py
@@ -223,6 +223,7 @@
         def attend(h):
             k_all = kvb[h, 0]
             v_all = kvb[h, 1]
+            v_ones = jnp.concatenate([v_all, jnp.ones_like(v_all)], axis=1)
             for g in range(0, group, PACK):
                 ats = [pl.ds(pl.multiple_of((h * group + g + n) * hd, hd), hd)
                        for n in range(PACK)]
@@ -233,9 +234,8 @@
                 s = jnp.concatenate([far, near], axis=1)
                 top = jnp.max(s, axis=1, keepdims=True)
                 w = jnp.exp2((s - top) * coef)
-                tot = jnp.sum(w, axis=1, keepdims=True)
-                o = jnp.dot(w.astype(bf16), v_all, preferred_element_type=f32)
-                o = (o * (1.0 / tot)).astype(bf16)
+                o = jnp.dot(w.astype(bf16), v_ones, preferred_element_type=f32)
+                o = (o[:, :hd] / o[:, hd:]).astype(bf16)
                 for n, at in enumerate(ats):
                     out_ref[:, at] = o[n * tok:(n + 1) * tok]
 

time: 27.2 us -> 26.9 us (0.989)
  Pallas kernels: 24.8 us -> 24.5 us
    pallas_call x1, Pallas kernels: 24.8 us -> 24.5 us  [body(): pl.pallas_call(kernel, out_shape=(pltpu.VMEM((tok, heads * hd), bf16), pl...]
where the time goes in v3:
time: 26.9 us; the launch traced here: 26.7 us
  Pallas kernels  24.5 us (91%)
  local copies, waits for them, and re-layouts  1.63 us (6%)
  between operations  0.64 us (2%)
    pallas_call x1, Pallas kernels, body(): pl.pallas_call(kernel, out_shape=(pltpu.VMEM((tok, heads * hd), bf16), pl...  24.5 us
    unnamed x2, local copies, waits for them, and re-layouts  1.63 us

profile of v3, /device:TPU:0, one launch (start us, length us, event | category | flops | bytes accessed | tf_op | source)
XLA Modules:
  0.0 26.7 jit_solution(157295272873830784)
XLA Ops:
  0.6 24.5 %shard_map.86 = (bf16[128,4096]{1,0:T(8,128)(2,1)S(1)}, bf16[12,4096]{1,0:T(8,128)(2,1)S(1)}) custom-call(s32[12]{0:T(128)} %len_ref.1, bf16[128,4096]{1,0:T(8,128)(2,1)} %q_hbm.1, bf16[128,1024]{1,0:T(8,128)(2,1)} %k_hbm.1, bf16[128,1024]{1,0:T(8,128)(2,1)} %v_hbm.1, bf16[12,4096]{1,0:T(8,128)(2,1)} %nq_hbm.1, bf16[12,1024]{1,0:T(8,128)(2,1)} %nk_hbm.1, ...), custom_call_target="tpu_custom_call" | custom-call | tf_op jit(solution)/shard_map/pallas_call | solution.py:324
  25.1 1.0 %copy.11 = bf16[128,4096]{1,0:T(8,128)(2,1)} copy(bf16[128,4096]{1,0:T(8,128)(2,1)S(1)} %get-tuple-element.2) | data formatting | bytes 2097152
  26.1 0.7 %copy.12 = bf16[12,4096]{1,0:T(8,128)(2,1)} copy(bf16[12,4096]{1,0:T(8,128)(2,1)S(1)} %get-tuple-element.3) | data formatting | bytes 196608
